TPU v7x, 256 devices: a whole 4x4x8 slice. The times are simulated.
256 devices in a mesh: freq: 32 (over z, x_lo, core), rcv: 8 (over x_hi, y).
Axes of the slice: x: 4 (x_hi: 2, x_lo: 2; x = x_hi * 2 + x_lo), y: 4, z: 8, core: 2. Of those that a mesh axis runs over, the one named last changes fastest.
Arguments:
- reflection: bfloat16 [2, 128, 768, 768], P(None, 'freq', 'rcv'), may hold values from -0.21875 to 0.21875
- direct: bfloat16 [768, 128, 512], P(('rcv', 'freq')), may hold values from -6 to 6
- onset: int32 [768, 128], P(('rcv', 'freq')), may hold values from 128 to 383
Outputs:
- focus_plus: bfloat16 [768, 128, 512], P(('rcv', 'freq'))
- focus_minus: bfloat16 [768, 128, 512], P(('rcv', 'freq'))
- correlation: float32 [2, 128, 128, 128], P(None, 'freq', 'rcv')
All inputs are finite; a program needn't handle non-finite values.
Results may differ from a plain program's by a relative error of at most 0.019.
Values may be sent and summed in bfloat16 or wider, within the bound.
No kernel may reach another device: no remote copies, remote signals or barrier semaphores. Data moves between devices by JAX's collectives and lax.ppermute only.
A program may use at most 64 MiB of HBM per device.

v0:
```python
import functools
import math

import jax
import jax.numpy as jnp
import ml_dtypes
import numpy as np
from jax import lax
from jax.experimental import pallas as pl
from jax.experimental.pallas import tpu as pltpu
from jax.sharding import Mesh
from jax.sharding import PartitionSpec as P

F32 = jnp.float32
BF16 = jnp.bfloat16
RCV = ("xh", "y")
OWNERS = ("xh", "y", "freq")
TRACES = ("y", "freq")


def fourier_table(samples, bins_of_owner):
    phase = (bins_of_owner[:, None] * np.arange(samples)[None, :]) % samples
    angle = 2.0 * math.pi / samples * phase
    rows = np.concatenate([np.cos(angle), -np.sin(angle)], axis=0) / math.sqrt(samples)
    return rows.astype(np.float32).astype(ml_dtypes.bfloat16)


def dot(a, b, da, db):
    return lax.dot_general(a, b, (((da,), (db,)), ((), ())), preferred_element_type=F32)


def run(kernel, out, scratch, *args, space=pltpu.VMEM, out_spaces=None):
    if out_spaces is None:
        out_spaces = jax.tree.map(lambda _: pltpu.VMEM, out)
    return pl.pallas_call(
        kernel,
        out_shape=out,
        in_specs=[pl.BlockSpec(memory_space=space)] * len(args),
        out_specs=jax.tree.map(lambda at: pl.BlockSpec(memory_space=at), out_spaces),
        scratch_shapes=scratch,
        compiler_params=pltpu.CompilerParams(
            vmem_limit_bytes=(63 if space == pltpu.HBM else 12) * 2**20
        ),
    )(*args)


def put_spectrum(field, table, rows_ref, i, step, conj):
    n = table.shape[0] // 2
    v = dot(table, field, 1, 1)
    rows_ref[pl.ds(2 * i, n, stride=step), :] = v[:n]
    im = v[n:]
    rows_ref[pl.ds(2 * i + 1, n, stride=step), :] = -im if conj else im


def flush(rows_ref, send_ref):
    rows = rows_ref[...].astype(BF16)
    for h in range(send_ref.shape[0]):
        send_ref[h] = rows


def open_kernel(reflection_hbm, direct_hbm, table_hbm, *refs):
    *block_hbms, send_ref, blocks_ref, direct_ref, table_ref, out_rows, in_sems, out_sems = refs
    n = direct_hbm.shape[0]
    y = lax.axis_index("y")
    whole = pltpu.make_async_copy(table_hbm, table_ref, in_sems.at[0])
    parts = [
        pltpu.make_async_copy(direct_hbm.at[i], direct_ref.at[i], in_sems.at[1 + i])
        for i in range(n)
    ]
    takes, puts = [], []
    for d, block_hbm in enumerate(block_hbms):
        at = jnp.bitwise_xor(y, d)
        sem = in_sems.at[1 + n + d]
        takes.append(pltpu.make_async_copy(reflection_hbm.at[:, at], blocks_ref.at[d], sem))
        puts.append(pltpu.make_async_copy(blocks_ref.at[d], block_hbm, out_sems.at[d]))
    for copy in (whole, *parts, *takes):
        copy.start()
    whole.wait()
    for i in range(n):
        parts[i].wait()
        put_spectrum(direct_ref[i], table_ref[...], out_rows, i, 2 * n, False)
        if i == 0:
            for take, put in zip(takes, puts):
                take.wait()
                put.start()
    flush(out_rows, send_ref)
    for put in puts:
        put.wait()


def trace_kernel(n, conj_in, conj_out, add, *refs):
    if add:
        got_ref, onset_ref, table_ref, direct_ref, field_ref, send_ref, in_rows, out_rows = refs
    else:
        got_ref, onset_ref, table_ref, field_ref, send_ref, in_rows, out_rows = refs
    table = table_ref[...]
    bins = table.shape[0] // 2
    step = 2 * n
    in_rows[...] = sum(got_ref[h].astype(F32) for h in range(1, got_ref.shape[0])) + got_ref[0].astype(F32)
    for i in range(n):
        re = in_rows[pl.ds(2 * i, bins, stride=step), :]
        im = in_rows[pl.ds(2 * i + 1, bins, stride=step), :]
        both = jnp.concatenate([re, -im if conj_in else im], axis=0).astype(BF16)
        trace = dot(both, table, 0, 0) * 2.0
        sample = lax.broadcasted_iota(jnp.int32, trace.shape, 1)
        square = (trace.shape[0], trace.shape[0])
        onset = jnp.broadcast_to(onset_ref[i : i + 1, :].astype(F32), square).T
        onset = jnp.concatenate([onset] * (trace.shape[1] // square[1]), axis=1)
        trace = jnp.where(sample.astype(F32) < onset, trace, 0.0)
        if add:
            trace = direct_ref[i].astype(F32) + trace
        field = trace.astype(BF16)
        field_ref[i] = field
        put_spectrum(field, table, out_rows, i, step, conj_out)
    flush(out_rows, send_ref)


def weave(even_odd, pieces, negate):
    for start, even, odd in pieces:
        block = even.shape[0]
        even_odd[pl.ds(start, block, stride=2), :] = even.astype(F32)
        odd = odd.astype(F32)
        even_odd[pl.ds(start + 1, block, stride=2), :] = -odd if negate else odd
    return even_odd[...].astype(BF16)


def weave_sources_kernel(*refs):
    *got_refs, w_ref, cut_ref, even_odd = refs
    _, block, receivers = got_refs[0].shape
    lanes = even_odd.shape[1]
    half = cut_ref.shape[3]
    other = pl.multiple_of((1 - lax.axis_index("xh")) * half, half)
    for d, ref in enumerate(got_refs):
        cut_ref[d] = ref[:, :, pl.ds(other, half)]
    y = lax.axis_index("y")
    starts = [2 * block * jnp.bitwise_xor(y, d) for d in range(len(got_refs))]
    for out in (0, 1):
        for col in range(0, receivers, lanes):
            pieces = [
                (start, ref[out, :, col : col + lanes], ref[1 - out, :, col : col + lanes])
                for start, ref in zip(starts, got_refs)
            ]
            at = out * receivers + col
            w_ref[:, at : at + lanes] = weave(even_odd, pieces, not out)


def weave_far_kernel(cut_ref, w_ref, even_odd):
    places, _, block, half = cut_ref.shape
    lanes = even_odd.shape[1]
    y = lax.axis_index("y")
    starts = [2 * block * jnp.bitwise_xor(y, d) for d in range(places)]
    for out in (0, 1):
        for col in range(0, half, lanes):
            cols = slice(col, col + lanes)
            pieces = [
                (start, cut_ref[d, out, :, cols], cut_ref[d, 1 - out, :, cols])
                for d, start in enumerate(starts)
            ]
            at = out * half + col
            w_ref[:, at : at + lanes] = weave(even_odd, pieces, not out)


def product(v_ref, w_ref):
    return dot(v_ref[...], w_ref[...], 0, 0).T


def apply_kernel(v_ref, w_ref, send_ref, rows):
    p = product(v_ref, w_ref)
    half = p.shape[0] // 2
    rows[pl.ds(0, half, stride=2), :] = p[:half]
    rows[pl.ds(1, half, stride=2), :] = p[half:]
    send_ref[...] = rows[...].astype(BF16)


def green_kernel(scale, v_ref, w_ref, far_ref, minus_ref, corr_ref, rows):
    rows[...] = minus_ref[...].astype(F32)
    half = far_ref.shape[1] // 2
    receivers = w_ref.shape[1] // 2
    xh = lax.axis_index("xh")
    own, far = v_ref[xh], v_ref[1 - xh]

    def part(c):
        cols = pl.ds(pl.multiple_of(c * receivers + xh * half, half), half)
        near = dot(own, w_ref[:, cols], 0, 0)
        return (near + dot(far, far_ref[:, c * half : (c + 1) * half], 0, 0)).T

    re = (part(0) - rows[pl.ds(0, half, stride=2), :]).astype(BF16)
    im = (part(1) + rows[pl.ds(1, half, stride=2), :]).astype(BF16)
    cross = dot(re, im, 0, 0)
    parts = (dot(re, re, 0, 0) + dot(im, im, 0, 0), cross - cross.T)
    peers, _, each, _ = corr_ref.shape
    for c, part in enumerate(parts):
        scaled = (part * scale).astype(BF16)
        for peer in range(peers):
            corr_ref[peer, c] = scaled[peer * each : (peer + 1) * each]


def total_kernel(got_ref, out_ref):
    bins = out_ref.shape[1]
    for c in range(out_ref.shape[0]):
        for k in range(bins):
            parts = [got_ref[at, c].astype(F32) for at in range(k, got_ref.shape[0], bins)]
            out_ref[c, k] = sum(parts[1:], parts[0])


def exchange(value, axes):
    return lax.all_to_all(value, axes, split_axis=0, concat_axis=0, tiled=True)


def on_device(reflection, direct, onset):
    n, focal, samples = direct.shape
    per_group = reflection.shape[1]
    block, receivers = reflection.shape[2:]
    halves, ys = lax.axis_size("xh"), lax.axis_size("y")
    groups = lax.axis_size("freq")
    bins = per_group * groups
    half = receivers // halves
    shape = jax.ShapeDtypeStruct

    order = (np.arange(groups)[None, :] * per_group + np.arange(ys)[:, None]).reshape(-1)
    table = jnp.asarray(fourier_table(samples, order))

    places = halves * ys
    rows_out = 2 * n * bins
    field_shape = shape(direct.shape, BF16)
    rows = pltpu.VMEM((rows_out, focal), F32)

    def send_shape(copies):
        return shape((copies, rows_out, focal), BF16)

    def swap(value, axes):
        parts = value.reshape(-1, n, 2, focal)
        return exchange(parts, axes).reshape(-1, rows_out, focal)

    piece = shape((2, block, receivers), BF16)
    *got, send = run(
        open_kernel,
        [piece] * ys + [send_shape(1)],
        [
            pltpu.VMEM((ys, *piece.shape), BF16),
            pltpu.VMEM(direct.shape, BF16),
            pltpu.VMEM(table.shape, BF16),
            rows,
            pltpu.SemaphoreType.DMA((1 + n + ys,)),
            pltpu.SemaphoreType.DMA((ys,)),
        ],
        reflection,
        direct,
        table,
        space=pltpu.HBM,
        out_spaces=[pltpu.HBM] * ys + [pltpu.VMEM],
    )
    for d in range(1, ys):
        got[d] = lax.ppermute(got[d], "y", [(j, j ^ d) for j in range(ys)])
    plus = swap(send, TRACES)
    w, cut = run(
        weave_sources_kernel,
        (shape((2 * half, 2 * receivers), BF16), shape((ys, 2, block, half), BF16)),
        [pltpu.VMEM((2 * half, focal), F32)],
        *got,
    )
    far = lax.ppermute(cut, "xh", [(j, j ^ 1) for j in range(halves)])
    w_far = run(
        weave_far_kernel,
        shape((2 * half, 2 * half), BF16),
        [pltpu.VMEM((2 * half, focal), F32)],
        far,
    )

    def apply(v):
        out = run(
            apply_kernel,
            shape((2 * receivers, focal), BF16),
            [pltpu.VMEM((2 * receivers, focal), F32)],
            v.reshape(2 * half, focal),
            w,
        )
        return swap(out, OWNERS)

    summed = apply(plus)
    focus_minus, send = run(
        functools.partial(trace_kernel, n, False, True, False),
        (field_shape, send_shape(1)),
        [rows, rows],
        summed,
        onset,
        table,
    )
    minus = swap(send, TRACES)
    summed = apply(minus)
    focus_plus, send = run(
        functools.partial(trace_kernel, n, True, False, True),
        (field_shape, send_shape(halves)),
        [rows, rows],
        summed,
        onset,
        table,
        direct,
    )
    plus = swap(send, OWNERS)
    each = focal // places
    parts = run(
        functools.partial(green_kernel, 1.0 / receivers),
        shape((places, 2, each, focal), BF16),
        [pltpu.VMEM((2 * half, focal), F32)],
        plus,
        w,
        w_far,
        minus.reshape(2 * half, focal),
    )
    correlation = run(
        total_kernel, shape((2, per_group, each, focal), F32), [], exchange(parts, RCV)
    )
    return focus_plus, focus_minus, correlation


def solution(mesh):
    groups, rcv = mesh.shape["freq"], mesh.shape["rcv"]
    fine = Mesh(mesh.devices.reshape(groups, 2, rcv // 2), ("freq", "xh", "y"))
    traces = ("xh", "y", "freq")
    return jax.shard_map(
        on_device,
        mesh=fine,
        in_specs=(P(None, "freq", RCV, None), P(traces, None, None), P(traces, None)),
        out_specs=(P(traces, None, None), P(traces, None, None), P(None, "freq", RCV, None)),
        check_vma=False,
    )
```

profile of v0, /device:TPU:2, one launch (start us, length us, event | category | flops | bytes accessed | tf_op | source)
XLA Modules:
  0.0 159.9 jit_solution(15061221952277369802)
XLA Ops:
  0.6 3.0 %shard_map.67 = (bf16[2,96,768]{2,1,0:T(8,128)(2,1)}, bf16[2,96,768]{2,1,0:T(8,128)(2,1)}, bf16[2,96,768]{2,1,0:T(8,128)(2,1)}, bf16[2,96,768]{2,1,0:T(8,128)(2,1)}, bf16[1,768,128]{2,1,0:T(8,128)(2,1)}) custom-call(bf16[2,4,96,768]{3,2,1,0:T(8,128)(2,1)} %reflection_hbm.1, bf16[3,128,512]{2,1,0:T(8,128)(2,1)} %refs_3_.1, ...), custom_call_target="tpu_custom_call" | custom-call | tf_op jit(solution)/shard_map/pallas_call | solution.py:35
  3.6 13.9 %all-to-all-start = ((bf16[128,3,2,128]{3,2,1,0:T(2,128)(2,1)}), bf16[128,3,2,128]{3,2,1,0:T(2,128)(2,1)S(1)}, u32[]{:S(2)}, u32[]{:S(2)}) async-start(bf16[128,3,2,128]{3,2,1,0:T(2,128)(2,1)} %bitcast.18), calls=%async_computation | async-start | bytes 393216 | tf_op jit(solution)/shard_map/all_to_all | solution.py:207
  17.5 1.7 %collective-permute-start = (bf16[2,96,768]{2,1,0:T(8,128)(2,1)}, bf16[2,96,768]{2,1,0:T(8,128)(2,1)S(1)}, u32[]{:S(2)}, u32[]{:S(2)}) collective-permute-start(bf16[2,96,768]{2,1,0:T(8,128)(2,1)} %get-tuple-element.16), channel_id=1, source_target_pairs={{0,1},{1,0},{2,3},{3,2},{4,5},{5,4},{6,7},{7,6},{8,9},{9,8},{10,11... | collective-permute-start | bytes 884744 | tf_op jit(solution)/shard_map/ppermute | solution.py:254
  19.2 3.1 %collective-permute-start.1 = (bf16[2,96,768]{2,1,0:T(8,128)(2,1)}, bf16[2,96,768]{2,1,0:T(8,128)(2,1)S(1)}, u32[]{:S(2)}, u32[]{:S(2)}) collective-permute-start(bf16[2,96,768]{2,1,0:T(8,128)(2,1)} %get-tuple-element.17), channel_id=1, source_target_pairs={{0,2},{1,3},{2,0},{3,1},{4,6},{5,7},{6,4},{7,5},{8,10},{9,11},{10,... | collective-permute-start | bytes 884744 | tf_op jit(solution)/shard_map/ppermute | solution.py:254
  22.3 0.0 collective-permute-start.2
  22.3 7.1 %collective-permute-done.refs_1_ = bf16[2,96,768]{2,1,0:T(8,128)(2,1)S(1)} collective-permute-done((bf16[2,96,768]{2,1,0:T(8,128)(2,1)}, bf16[2,96,768]{2,1,0:T(8,128)(2,1)S(1)}, u32[]{:S(2)}, u32[]{:S(2)}) %collective-permute-start) | collective-permute-done | bytes 294944 | tf_op jit(solution)/shard_map/ppermute | solution.py:254
  29.4 8.1 %collective-permute-done.1.refs_2_ = bf16[2,96,768]{2,1,0:T(8,128)(2,1)S(1)} collective-permute-done((bf16[2,96,768]{2,1,0:T(8,128)(2,1)}, bf16[2,96,768]{2,1,0:T(8,128)(2,1)S(1)}, u32[]{:S(2)}, u32[]{:S(2)}) %collective-permute-start.1) | collective-permute-done | bytes 294944 | tf_op jit(solution)/shard_map/ppermute | solution.py:254
  37.5 1.6 %collective-permute-done.2.refs_3_ = bf16[2,96,768]{2,1,0:T(8,128)(2,1)S(1)} collective-permute-done((bf16[2,96,768]{2,1,0:T(8,128)(2,1)}, bf16[2,96,768]{2,1,0:T(8,128)(2,1)S(1)}, u32[]{:S(2)}, u32[]{:S(2)}) %collective-permute-start.2) | collective-permute-done | bytes 294944 | tf_op jit(solution)/shard_map/ppermute | solution.py:254
  39.2 0.0 copy-start.4
  39.2 1.0 copy-done.4
  40.1 0.8 shard_map.68
  41.0 0.0 all-to-all-done
  41.0 0.0 copy-start
  41.0 0.0 copy-start.5
  41.0 0.6 shard_map.69
  41.7 26.9 %all_to_all.30 = bf16[256,3,2,128]{3,2,1,0:T(2,128)(2,1)S(1)} all-to-all(bf16[256,3,2,128]{3,2,1,0:T(2,128)(2,1)S(1)} %bitcast.14), channel_id=1, replica_groups=mesh['freq'=32,'xh'=2,'y'=4] {'xh','y','freq'}, dimensions={0} | all-to-all | bytes 786432 | tf_op jit(solution)/shard_map/all_to_all | solution.py:207
  68.6 0.0 copy-done
  68.6 0.0 copy-done.5
  68.6 1.3 shard_map.70
  69.9 18.6 %all_to_all.31 = bf16[128,3,2,128]{3,2,1,0:T(2,128)(2,1)S(1)} all-to-all(bf16[128,3,2,128]{3,2,1,0:T(2,128)(2,1)S(1)} %bitcast.17), channel_id=1, replica_groups=mesh['freq'=32,'xh'=2,'y'=4] {'y','freq'}, dimensions={0} | all-to-all | bytes 393216 | tf_op jit(solution)/shard_map/all_to_all | solution.py:207
  88.5 0.0 copy-start.1
  88.5 0.0 copy-start.3
  88.5 0.7 shard_map.71
  89.1 0.0 copy-done.1
  89.1 23.5 %all_to_all.32 = bf16[256,3,2,128]{3,2,1,0:T(2,128)(2,1)S(1)} all-to-all(bf16[256,3,2,128]{3,2,1,0:T(2,128)(2,1)S(1)} %bitcast.15), channel_id=1, replica_groups=mesh['freq'=32,'xh'=2,'y'=4] {'xh','y','freq'}, dimensions={0} | all-to-all | bytes 786432 | tf_op jit(solution)/shard_map/all_to_all | solution.py:207
  112.6 0.0 copy-done.3
  112.6 1.6 shard_map.72
  114.2 8.1 %all-to-all-start.4 = ((bf16[256,3,2,128]{3,2,1,0:T(2,128)(2,1)}), bf16[256,3,2,128]{3,2,1,0:T(2,128)(2,1)}, u32[]{:S(2)}, u32[]{:S(2)}) async-start(bf16[256,3,2,128]{3,2,1,0:T(2,128)(2,1)} %bitcast.8), calls=%async_computation.4 | async-start | bytes 786432 | tf_op jit(solution)/shard_map/all_to_all | solution.py:207
  122.3 2.2 %collective-permute-start.3 = (bf16[4,2,96,384]{3,2,1,0:T(8,128)(2,1)S(1)}, bf16[4,2,96,384]{3,2,1,0:T(8,128)(2,1)S(1)}, u32[]{:S(2)}, u32[]{:S(2)}) collective-permute-start(bf16[4,2,96,384]{3,2,1,0:T(8,128)(2,1)S(1)} %get-tuple-element.24), channel_id=1, source_target_pairs={{0,4},{4,0},{1,5},{5,1},{2,6},{6,2},{3,7},{7,3},{8,12},{12,8},{9,1... | collective-permute-start | bytes 1769480 | tf_op jit(solution)/shard_map/ppermute | solution.py:262
  124.5 18.0 %collective-permute-done.3.cut_ref = bf16[4,2,96,384]{3,2,1,0:T(8,128)(2,1)S(1)} collective-permute-done((bf16[4,2,96,384]{3,2,1,0:T(8,128)(2,1)S(1)}, bf16[4,2,96,384]{3,2,1,0:T(8,128)(2,1)S(1)}, u32[]{:S(2)}, u32[]{:S(2)}) %collective-permute-start.3) | collective-permute-done | bytes 589856 | tf_op jit(solution)/shard_map/ppermute | solution.py:262
  142.5 0.4 shard_map.73.far_ref
  142.9 0.0 all-to-all-done.4
  142.9 0.0 copy-start.2
  142.9 0.9 copy-done.2
  143.8 2.0 %shard_map.74 = bf16[8,2,16,128]{3,2,1,0:T(8,128)(2,1)S(1)} custom-call(bf16[2,768,128]{2,1,0:T(8,128)(2,1)} %bitcast.9.v_ref, bf16[768,1536]{1,0:T(8,128)(2,1)S(1)} %get-tuple-element.19.w_ref, bf16[768,768]{1,0:T(8,128)(2,1)S(1)} %shard_map.73.far_ref, bf16[768,128]{1,0:T(8,128)(2,1)S(1)} %bitcast.11), custom_call_target="tpu_custom_call" | custom-call | tf_op jit(solution)/shard_map/pallas_call | solution.py:35
  145.8 13.4 %all_to_all.33.got_ref = bf16[8,2,16,128]{3,2,1,0:T(8,128)(2,1)S(1)} all-to-all(bf16[8,2,16,128]{3,2,1,0:T(8,128)(2,1)S(1)} %shard_map.74), channel_id=1, replica_groups=mesh['freq'=32,'xh'=2,'y'=4] {'xh','y'}, dimensions={0} | all-to-all | bytes 131072 | tf_op jit(solution)/shard_map/all_to_all | solution.py:207
  159.2 0.6 shard_map.75
Async XLA Ops:
  3.6 37.3 %all-to-all-start = ((bf16[128,3,2,128]{3,2,1,0:T(2,128)(2,1)}), bf16[128,3,2,128]{3,2,1,0:T(2,128)(2,1)S(1)}, u32[]{:S(2)}, u32[]{:S(2)}) async-start(bf16[128,3,2,128]{3,2,1,0:T(2,128)(2,1)} %bitcast.18), calls=%async_computation | async-start | bytes 393216 | tf_op jit(solution)/shard_map/all_to_all | solution.py:207
  17.5 11.9 %collective-permute-start = (bf16[2,96,768]{2,1,0:T(8,128)(2,1)}, bf16[2,96,768]{2,1,0:T(8,128)(2,1)S(1)}, u32[]{:S(2)}, u32[]{:S(2)}) collective-permute-start(bf16[2,96,768]{2,1,0:T(8,128)(2,1)} %get-tuple-element.16), channel_id=1, source_target_pairs={{0,1},{1,0},{2,3},{3,2},{4,5},{5,4},{6,7},{7,6},{8,9},{9,8},{10,11... | collective-permute-start | bytes 884744 | tf_op jit(solution)/shard_map/ppermute | solution.py:254
  19.2 18.3 %collective-permute-start.1 = (bf16[2,96,768]{2,1,0:T(8,128)(2,1)}, bf16[2,96,768]{2,1,0:T(8,128)(2,1)S(1)}, u32[]{:S(2)}, u32[]{:S(2)}) collective-permute-start(bf16[2,96,768]{2,1,0:T(8,128)(2,1)} %get-tuple-element.17), channel_id=1, source_target_pairs={{0,2},{1,3},{2,0},{3,1},{4,6},{5,7},{6,4},{7,5},{8,10},{9,11},{10,... | collective-permute-start | bytes 884744 | tf_op jit(solution)/shard_map/ppermute | solution.py:254
  22.3 16.9 %collective-permute-start.2 = (bf16[2,96,768]{2,1,0:T(8,128)(2,1)}, bf16[2,96,768]{2,1,0:T(8,128)(2,1)S(1)}, u32[]{:S(2)}, u32[]{:S(2)}) collective-permute-start(bf16[2,96,768]{2,1,0:T(8,128)(2,1)} %get-tuple-element.18), channel_id=1, source_target_pairs={{0,3},{1,2},{2,1},{3,0},{4,7},{5,6},{6,5},{7,4},{8,11},{9,10},{10,... | collective-permute-start | bytes 884744 | tf_op jit(solution)/shard_map/ppermute | solution.py:254
  39.2 1.0 copy-start.4
  41.0 27.6 %copy-start = (bf16[256,512]{1,0:T(8,128)(2,1)S(1)}, bf16[256,512]{1,0:T(8,128)(2,1)}, u32[]{:S(2)}) copy-start(bf16[256,512]{1,0:T(8,128)(2,1)} %constant.2.clone.table_hbm.refs_2_) | copy-start | bytes 786436
  41.0 27.6 %copy-start.5 = (s32[3,128]{1,0:T(4,128)S(1)}, s32[3,128]{1,0:T(4,128)}, u32[]{:S(2)}) copy-start(s32[3,128]{1,0:T(4,128)} %refs_1_.3) | copy-start | bytes 4612
  88.5 0.7 copy-start.1
  88.5 24.1 %copy-start.3 = (bf16[3,128,512]{2,1,0:T(8,128)(2,1)S(1)}, bf16[3,128,512]{2,1,0:T(8,128)(2,1)}, u32[]{:S(2)}) copy-start(bf16[3,128,512]{2,1,0:T(8,128)(2,1)} %refs_3_.1) | copy-start | bytes 1179652
  114.2 28.7 %all-to-all-start.4 = ((bf16[256,3,2,128]{3,2,1,0:T(2,128)(2,1)}), bf16[256,3,2,128]{3,2,1,0:T(2,128)(2,1)}, u32[]{:S(2)}, u32[]{:S(2)}) async-start(bf16[256,3,2,128]{3,2,1,0:T(2,128)(2,1)} %bitcast.8), calls=%async_computation.4 | async-start | bytes 786432 | tf_op jit(solution)/shard_map/all_to_all | solution.py:207
  122.3 20.2 %collective-permute-start.3 = (bf16[4,2,96,384]{3,2,1,0:T(8,128)(2,1)S(1)}, bf16[4,2,96,384]{3,2,1,0:T(8,128)(2,1)S(1)}, u32[]{:S(2)}, u32[]{:S(2)}) collective-permute-start(bf16[4,2,96,384]{3,2,1,0:T(8,128)(2,1)S(1)} %get-tuple-element.24), channel_id=1, source_target_pairs={{0,4},{4,0},{1,5},{5,1},{2,6},{6,2},{3,7},{7,3},{8,12},{12,8},{9,1... | collective-permute-start | bytes 1769480 | tf_op jit(solution)/shard_map/ppermute | solution.py:262
  142.9 0.9 copy-start.2
where the time goes:
time: 160 us
  blocking collectives  82.4 us (52%)
  waiting for transfers between devices  34.8 us (22%)
  starting transfers between devices  29 us (18%)
  Pallas kernels  11 us (7%)
  local copies, waits for them, and re-layouts  1.92 us (1%)
    all_to_all x4, blocking collectives, exchange(): return lax.all_to_all(value, axes, split_axis=0, concat_axis=0, tiled=True)  82.4 us
    all_to_all x2, starting transfers between devices, exchange(): return lax.all_to_all(value, axes, split_axis=0, concat_axis=0, tiled=True)  22 us
    ppermute x1, waiting for transfers between devices, on_device(): far = lax.ppermute(cut, 'xh', [(j, j ^ 1) for j in range(halves)])  18 us
    ppermute x3, waiting for transfers between devices, on_device(): got[d] = lax.ppermute(got[d], 'y', [(j, j ^ d) for j in range(ys)])  16.9 us
    pallas_call x9, Pallas kernels, run(): pl.pallas_call(kernel, out_shape=out, in_specs=[pl.BlockSpec(memory_space...  11 us
    ppermute x3, starting transfers between devices, on_device(): got[d] = lax.ppermute(got[d], 'y', [(j, j ^ d) for j in range(ys)])  4.79 us
  transfers between devices with their start and end apart: 6, of which 4 were waited for; matrix products, arithmetic and copies ran while one was open for 0% of the time, Pallas kernels for 1%

commit v1 on v0

--- a/solution.py
+++ b/solution.py
@@ -89,14 +89,16 @@
 
 
 def trace_kernel(n, conj_in, conj_out, add, *refs):
-    if add:
-        got_ref, onset_ref, table_ref, direct_ref, field_ref, send_ref, in_rows, out_rows = refs
-    else:
-        got_ref, onset_ref, table_ref, field_ref, send_ref, in_rows, out_rows = refs
+    got_ref, onset_ref, table_ref, *refs = refs
+    direct_ref = refs.pop(0) if add else None
+    field_hbm, send_ref, field_ref, in_rows, out_rows, sems = refs
     table = table_ref[...]
     bins = table.shape[0] // 2
     step = 2 * n
-    in_rows[...] = sum(got_ref[h].astype(F32) for h in range(1, got_ref.shape[0])) + got_ref[0].astype(F32)
+    summed = got_ref[0].astype(F32)
+    for h in range(1, got_ref.shape[0]):
+        summed += got_ref[h].astype(F32)
+    in_rows[...] = summed
     for i in range(n):
         re = in_rows[pl.ds(2 * i, bins, stride=step), :]
         im = in_rows[pl.ds(2 * i + 1, bins, stride=step), :]
@@ -109,10 +111,16 @@
         trace = jnp.where(sample.astype(F32) < onset, trace, 0.0)
         if add:
             trace = direct_ref[i].astype(F32) + trace
-        field = trace.astype(BF16)
-        field_ref[i] = field
-        put_spectrum(field, table, out_rows, i, step, conj_out)
+        field_ref[i] = trace.astype(BF16)
+    put_spectrum(field_ref[0], table, out_rows, 0, step, conj_out)
+    copies = [pltpu.make_async_copy(field_ref.at[i], field_hbm.at[i], sems.at[i]) for i in range(n)]
+    for copy in copies:
+        copy.start()
+    for i in range(1, n):
+        put_spectrum(field_ref[i], table, out_rows, i, step, conj_out)
     flush(out_rows, send_ref)
+    for copy in copies:
+        copy.wait()
 
 
 def weave(even_odd, pieces, negate):
@@ -260,12 +268,6 @@
         *got,
     )
     far = lax.ppermute(cut, "xh", [(j, j ^ 1) for j in range(halves)])
-    w_far = run(
-        weave_far_kernel,
-        shape((2 * half, 2 * half), BF16),
-        [pltpu.VMEM((2 * half, focal), F32)],
-        far,
-    )
 
     def apply(v):
         out = run(
@@ -277,26 +279,31 @@
         )
         return swap(out, OWNERS)
 
+    def to_field(summed, conj, copies, *extra):
+        return run(
+            functools.partial(trace_kernel, n, not conj, conj, bool(extra)),
+            (field_shape, send_shape(copies)),
+            [pltpu.VMEM(direct.shape, BF16), rows, rows, pltpu.SemaphoreType.DMA((n,))],
+            summed,
+            onset,
+            table,
+            *extra,
+            out_spaces=(pltpu.HBM, pltpu.VMEM),
+        )
+
     summed = apply(plus)
-    focus_minus, send = run(
-        functools.partial(trace_kernel, n, False, True, False),
-        (field_shape, send_shape(1)),
-        [rows, rows],
-        summed,
-        onset,
-        table,
-    )
+    focus_minus, send = to_field(summed, True, 1)
+    send, far = lax.optimization_barrier((send, far))
+    w_far = run(
+        weave_far_kernel,
+        shape((2 * half, 2 * half), BF16),
+        [pltpu.VMEM((2 * half, focal), F32)],
+        far,
+    )
+    send, w_far = lax.optimization_barrier((send, w_far))
     minus = swap(send, TRACES)
     summed = apply(minus)
-    focus_plus, send = run(
-        functools.partial(trace_kernel, n, True, False, True),
-        (field_shape, send_shape(halves)),
-        [rows, rows],
-        summed,
-        onset,
-        table,
-        direct,
-    )
+    focus_plus, send = to_field(summed, False, halves, direct)
     plus = swap(send, OWNERS)
     each = focal // places
     parts = run(

time: 160 us -> 162 us (1.012)
    ppermute x1, waiting for transfers between devices: 18 us -> 1.69 us  [on_device(): far = lax.ppermute(cut, 'xh', [(j, j ^ 1) for j in range(halves)])]
    all_to_all x2, waiting for transfers between devices: 0.01 us -> 15.5 us  [exchange(): return lax.all_to_all(value, axes, split_axis=0, concat_axis=0, tiled=True)]
  transfers between devices with their start and end apart: 6 -> 6, of which waited for: 4 -> 5; matrix products, arithmetic and copies ran while one was open for 0% -> 0% of each run, Pallas kernels for 1% -> 1%
where the time goes in v1:
time: 162 us; the launch traced here: 161 us
  blocking collectives  82.4 us (51%)
  waiting for transfers between devices  34 us (21%)
  starting transfers between devices  30.3 us (19%)
  Pallas kernels  11.4 us (7%)
  local copies, waits for them, and re-layouts  1.78 us (1%)
    all_to_all x4, blocking collectives, exchange(): return lax.all_to_all(value, axes, split_axis=0, concat_axis=0, tiled=True)  82.4 us
    all_to_all x2, starting transfers between devices, exchange(): return lax.all_to_all(value, axes, split_axis=0, concat_axis=0, tiled=True)  23.4 us
    ppermute x3, waiting for transfers between devices, on_device(): got[d] = lax.ppermute(got[d], 'y', [(j, j ^ d) for j in range(ys)])  16.9 us
    all_to_all x2, waiting for transfers between devices, exchange(): return lax.all_to_all(value, axes, split_axis=0, concat_axis=0, tiled=True)  15.5 us
    pallas_call x9, Pallas kernels, run(): pl.pallas_call(kernel, out_shape=out, in_specs=[pl.BlockSpec(memory_space...  11.4 us
    ppermute x3, starting transfers between devices, on_device(): got[d] = lax.ppermute(got[d], 'y', [(j, j ^ d) for j in range(ys)])  4.79 us
  transfers between devices with their start and end apart: 6, of which 5 were waited for; matrix products, arithmetic and copies ran while one was open for 0% of the time, Pallas kernels for 1%

profile of v1, /device:TPU:2, one launch (start us, length us, event | category | flops | bytes accessed | tf_op | source)
XLA Modules:
  0.0 160.7 jit_solution(15609432043029873637)
XLA Ops:
  0.6 3.0 %shard_map.67 = (bf16[2,96,768]{2,1,0:T(8,128)(2,1)}, bf16[2,96,768]{2,1,0:T(8,128)(2,1)}, bf16[2,96,768]{2,1,0:T(8,128)(2,1)}, bf16[2,96,768]{2,1,0:T(8,128)(2,1)}, bf16[1,768,128]{2,1,0:T(8,128)(2,1)}) custom-call(bf16[2,4,96,768]{3,2,1,0:T(8,128)(2,1)} %reflection_hbm.1, bf16[3,128,512]{2,1,0:T(8,128)(2,1)} %refs_3_.1, ...), custom_call_target="tpu_custom_call" | custom-call | tf_op jit(solution)/shard_map/pallas_call | solution.py:35
  3.6 13.9 %all-to-all-start = ((bf16[128,3,2,128]{3,2,1,0:T(2,128)(2,1)}), bf16[128,3,2,128]{3,2,1,0:T(2,128)(2,1)S(1)}, u32[]{:S(2)}, u32[]{:S(2)}) async-start(bf16[128,3,2,128]{3,2,1,0:T(2,128)(2,1)} %bitcast.19), calls=%async_computation | async-start | bytes 393216 | tf_op jit(solution)/shard_map/all_to_all | solution.py:215
  17.5 1.7 %collective-permute-start = (bf16[2,96,768]{2,1,0:T(8,128)(2,1)}, bf16[2,96,768]{2,1,0:T(8,128)(2,1)S(1)}, u32[]{:S(2)}, u32[]{:S(2)}) collective-permute-start(bf16[2,96,768]{2,1,0:T(8,128)(2,1)} %get-tuple-element.20), channel_id=1, source_target_pairs={{0,1},{1,0},{2,3},{3,2},{4,5},{5,4},{6,7},{7,6},{8,9},{9,8},{10,11... | collective-permute-start | bytes 884744 | tf_op jit(solution)/shard_map/ppermute | solution.py:262
  19.2 3.1 %collective-permute-start.1 = (bf16[2,96,768]{2,1,0:T(8,128)(2,1)}, bf16[2,96,768]{2,1,0:T(8,128)(2,1)S(1)}, u32[]{:S(2)}, u32[]{:S(2)}) collective-permute-start(bf16[2,96,768]{2,1,0:T(8,128)(2,1)} %get-tuple-element.21), channel_id=1, source_target_pairs={{0,2},{1,3},{2,0},{3,1},{4,6},{5,7},{6,4},{7,5},{8,10},{9,11},{10,... | collective-permute-start | bytes 884744 | tf_op jit(solution)/shard_map/ppermute | solution.py:262
  22.3 0.0 collective-permute-start.2
  22.3 7.1 %collective-permute-done.refs_1_ = bf16[2,96,768]{2,1,0:T(8,128)(2,1)S(1)} collective-permute-done((bf16[2,96,768]{2,1,0:T(8,128)(2,1)}, bf16[2,96,768]{2,1,0:T(8,128)(2,1)S(1)}, u32[]{:S(2)}, u32[]{:S(2)}) %collective-permute-start) | collective-permute-done | bytes 294944 | tf_op jit(solution)/shard_map/ppermute | solution.py:262
  29.4 8.1 %collective-permute-done.1.refs_2_ = bf16[2,96,768]{2,1,0:T(8,128)(2,1)S(1)} collective-permute-done((bf16[2,96,768]{2,1,0:T(8,128)(2,1)}, bf16[2,96,768]{2,1,0:T(8,128)(2,1)S(1)}, u32[]{:S(2)}, u32[]{:S(2)}) %collective-permute-start.1) | collective-permute-done | bytes 294944 | tf_op jit(solution)/shard_map/ppermute | solution.py:262
  37.5 1.6 %collective-permute-done.2.refs_3_ = bf16[2,96,768]{2,1,0:T(8,128)(2,1)S(1)} collective-permute-done((bf16[2,96,768]{2,1,0:T(8,128)(2,1)}, bf16[2,96,768]{2,1,0:T(8,128)(2,1)S(1)}, u32[]{:S(2)}, u32[]{:S(2)}) %collective-permute-start.2) | collective-permute-done | bytes 294944 | tf_op jit(solution)/shard_map/ppermute | solution.py:262
  39.2 0.0 copy-start.2
  39.2 1.0 copy-done.2
  40.1 0.8 shard_map.68
  41.0 0.0 copy-start.4
  41.0 0.8 copy-done.4
  41.8 0.0 all-to-all-done
  41.8 0.0 copy-start
  41.8 0.0 copy-start.3
  41.8 1.4 shard_map.69
  43.2 9.5 %all-to-all-start.1 = ((bf16[256,3,2,128]{3,2,1,0:T(2,128)(2,1)}), bf16[256,3,2,128]{3,2,1,0:T(2,128)(2,1)S(1)}, u32[]{:S(2)}, u32[]{:S(2)}) async-start(bf16[256,3,2,128]{3,2,1,0:T(2,128)(2,1)} %bitcast.2), calls=%async_computation.1 | async-start | bytes 786432 | tf_op jit(solution)/shard_map/all_to_all | solution.py:215
  52.7 2.2 %collective-permute-start.3 = (bf16[4,2,96,384]{3,2,1,0:T(8,128)(2,1)}, bf16[4,2,96,384]{3,2,1,0:T(8,128)(2,1)}, u32[]{:S(2)}, u32[]{:S(2)}) collective-permute-start(bf16[4,2,96,384]{3,2,1,0:T(8,128)(2,1)} %copy-done.4), channel_id=1, source_target_pairs={{0,4},{4,0},{1,5},{5,1},{2,6},{6,2},{3,7},{7,3},{8,12},{12,8},{9,1... | collective-permute-start | bytes 1769480 | tf_op jit(solution)/shard_map/ppermute | solution.py:270
  54.8 15.5 %all-to-all-done.1 = bf16[256,3,2,128]{3,2,1,0:T(2,128)(2,1)S(1)} async-done(((bf16[256,3,2,128]{3,2,1,0:T(2,128)(2,1)}), bf16[256,3,2,128]{3,2,1,0:T(2,128)(2,1)S(1)}, u32[]{:S(2)}, u32[]{:S(2)}) %all-to-all-start.1) | async-done | bytes 393248 | tf_op jit(solution)/shard_map/all_to_all | solution.py:215
  70.3 0.0 copy-done
  70.3 0.0 copy-done.3
  70.3 1.2 shard_map.70
  71.6 1.7 %collective-permute-done.3.cut_ref = bf16[4,2,96,384]{3,2,1,0:T(8,128)(2,1)} collective-permute-done((bf16[4,2,96,384]{3,2,1,0:T(8,128)(2,1)}, bf16[4,2,96,384]{3,2,1,0:T(8,128)(2,1)}, u32[]{:S(2)}, u32[]{:S(2)}) %collective-permute-start.3) | collective-permute-done | bytes 589856 | tf_op jit(solution)/shard_map/ppermute | solution.py:270
  73.3 1.4 shard_map.71.far_ref
  74.7 23.9 %all_to_all.30 = bf16[128,3,2,128]{3,2,1,0:T(2,128)(2,1)S(1)} all-to-all(bf16[128,3,2,128]{3,2,1,0:T(2,128)(2,1)S(1)} %bitcast.18), channel_id=1, replica_groups=mesh['freq'=32,'xh'=2,'y'=4] {'y','freq'}, dimensions={0} | all-to-all | bytes 393216 | tf_op jit(solution)/shard_map/all_to_all | solution.py:215
  98.6 0.0 copy-start.1
  98.6 0.6 shard_map.72
  99.3 24.1 %all_to_all.31 = bf16[256,3,2,128]{3,2,1,0:T(2,128)(2,1)S(1)} all-to-all(bf16[256,3,2,128]{3,2,1,0:T(2,128)(2,1)S(1)} %bitcast.15), channel_id=1, replica_groups=mesh['freq'=32,'xh'=2,'y'=4] {'xh','y','freq'}, dimensions={0} | all-to-all | bytes 786432 | tf_op jit(solution)/shard_map/all_to_all | solution.py:215
  123.4 0.0 copy-done.1
  123.4 1.3 shard_map.73
  124.7 24.0 %all_to_all.32 = bf16[256,3,2,128]{3,2,1,0:T(2,128)(2,1)S(1)} all-to-all(bf16[256,3,2,128]{3,2,1,0:T(2,128)(2,1)S(1)} %bitcast.17), channel_id=1, replica_groups=mesh['freq'=32,'xh'=2,'y'=4] {'xh','y','freq'}, dimensions={0} | all-to-all | bytes 786432 | tf_op jit(solution)/shard_map/all_to_all | solution.py:215
  148.7 1.0 shard_map.74
  149.7 10.4 %all_to_all.33.got_ref = bf16[8,2,16,128]{3,2,1,0:T(8,128)(2,1)S(1)} all-to-all(bf16[8,2,16,128]{3,2,1,0:T(8,128)(2,1)S(1)} %shard_map.74), channel_id=1, replica_groups=mesh['freq'=32,'xh'=2,'y'=4] {'xh','y'}, dimensions={0} | all-to-all | bytes 131072 | tf_op jit(solution)/shard_map/all_to_all | solution.py:215
  160.1 0.6 shard_map.75
Async XLA Ops:
  3.6 38.2 %all-to-all-start = ((bf16[128,3,2,128]{3,2,1,0:T(2,128)(2,1)}), bf16[128,3,2,128]{3,2,1,0:T(2,128)(2,1)S(1)}, u32[]{:S(2)}, u32[]{:S(2)}) async-start(bf16[128,3,2,128]{3,2,1,0:T(2,128)(2,1)} %bitcast.19), calls=%async_computation | async-start | bytes 393216 | tf_op jit(solution)/shard_map/all_to_all | solution.py:215
  17.5 11.9 %collective-permute-start = (bf16[2,96,768]{2,1,0:T(8,128)(2,1)}, bf16[2,96,768]{2,1,0:T(8,128)(2,1)S(1)}, u32[]{:S(2)}, u32[]{:S(2)}) collective-permute-start(bf16[2,96,768]{2,1,0:T(8,128)(2,1)} %get-tuple-element.20), channel_id=1, source_target_pairs={{0,1},{1,0},{2,3},{3,2},{4,5},{5,4},{6,7},{7,6},{8,9},{9,8},{10,11... | collective-permute-start | bytes 884744 | tf_op jit(solution)/shard_map/ppermute | solution.py:262
  19.2 18.3 %collective-permute-start.1 = (bf16[2,96,768]{2,1,0:T(8,128)(2,1)}, bf16[2,96,768]{2,1,0:T(8,128)(2,1)S(1)}, u32[]{:S(2)}, u32[]{:S(2)}) collective-permute-start(bf16[2,96,768]{2,1,0:T(8,128)(2,1)} %get-tuple-element.21), channel_id=1, source_target_pairs={{0,2},{1,3},{2,0},{3,1},{4,6},{5,7},{6,4},{7,5},{8,10},{9,11},{10,... | collective-permute-start | bytes 884744 | tf_op jit(solution)/shard_map/ppermute | solution.py:262
  22.3 16.9 %collective-permute-start.2 = (bf16[2,96,768]{2,1,0:T(8,128)(2,1)}, bf16[2,96,768]{2,1,0:T(8,128)(2,1)S(1)}, u32[]{:S(2)}, u32[]{:S(2)}) collective-permute-start(bf16[2,96,768]{2,1,0:T(8,128)(2,1)} %get-tuple-element.22), channel_id=1, source_target_pairs={{0,3},{1,2},{2,1},{3,0},{4,7},{5,6},{6,5},{7,4},{8,11},{9,10},{10,... | collective-permute-start | bytes 884744 | tf_op jit(solution)/shard_map/ppermute | solution.py:262
  39.2 1.0 copy-start.2
  41.0 0.8 copy-start.4
  41.8 28.5 %copy-start = (bf16[256,512]{1,0:T(8,128)(2,1)S(1)}, bf16[256,512]{1,0:T(8,128)(2,1)}, u32[]{:S(2)}) copy-start(bf16[256,512]{1,0:T(8,128)(2,1)} %constant.2.clone.table_hbm.refs_2_) | copy-start | bytes 786436
  41.8 28.5 %copy-start.3 = (s32[3,128]{1,0:T(4,128)S(1)}, s32[3,128]{1,0:T(4,128)}, u32[]{:S(2)}) copy-start(s32[3,128]{1,0:T(4,128)} %refs_1_.3) | copy-start | bytes 4612
  43.2 27.1 %all-to-all-start.1 = ((bf16[256,3,2,128]{3,2,1,0:T(2,128)(2,1)}), bf16[256,3,2,128]{3,2,1,0:T(2,128)(2,1)S(1)}, u32[]{:S(2)}, u32[]{:S(2)}) async-start(bf16[256,3,2,128]{3,2,1,0:T(2,128)(2,1)} %bitcast.2), calls=%async_computation.1 | async-start | bytes 786432 | tf_op jit(solution)/shard_map/all_to_all | solution.py:215
  52.7 20.6 %collective-permute-start.3 = (bf16[4,2,96,384]{3,2,1,0:T(8,128)(2,1)}, bf16[4,2,96,384]{3,2,1,0:T(8,128)(2,1)}, u32[]{:S(2)}, u32[]{:S(2)}) collective-permute-start(bf16[4,2,96,384]{3,2,1,0:T(8,128)(2,1)} %copy-done.4), channel_id=1, source_target_pairs={{0,4},{4,0},{1,5},{5,1},{2,6},{6,2},{3,7},{7,3},{8,12},{12,8},{9,1... | collective-permute-start | bytes 1769480 | tf_op jit(solution)/shard_map/ppermute | solution.py:270
  98.6 24.8 %copy-start.1 = (bf16[3,128,512]{2,1,0:T(8,128)(2,1)S(1)}, bf16[3,128,512]{2,1,0:T(8,128)(2,1)}, u32[]{:S(2)}) copy-start(bf16[3,128,512]{2,1,0:T(8,128)(2,1)} %refs_3_.1) | copy-start | bytes 1179652

commit v2 on v1

--- a/solution.py
+++ b/solution.py
@@ -91,7 +91,7 @@
 def trace_kernel(n, conj_in, conj_out, add, *refs):
     got_ref, onset_ref, table_ref, *refs = refs
     direct_ref = refs.pop(0) if add else None
-    field_hbm, send_ref, field_ref, in_rows, out_rows, sems = refs
+    field_ref, send_ref, in_rows, out_rows = refs
     table = table_ref[...]
     bins = table.shape[0] // 2
     step = 2 * n
@@ -112,15 +112,8 @@
         if add:
             trace = direct_ref[i].astype(F32) + trace
         field_ref[i] = trace.astype(BF16)
-    put_spectrum(field_ref[0], table, out_rows, 0, step, conj_out)
-    copies = [pltpu.make_async_copy(field_ref.at[i], field_hbm.at[i], sems.at[i]) for i in range(n)]
-    for copy in copies:
-        copy.start()
-    for i in range(1, n):
         put_spectrum(field_ref[i], table, out_rows, i, step, conj_out)
     flush(out_rows, send_ref)
-    for copy in copies:
-        copy.wait()
 
 
 def weave(even_odd, pieces, negate):
@@ -180,7 +173,14 @@
     send_ref[...] = rows[...].astype(BF16)
 
 
-def green_kernel(scale, v_ref, w_ref, far_ref, minus_ref, corr_ref, rows):
+def green_kernel(scale, *refs):
+    v_ref, w_ref, far_ref, minus_ref, *fields, corr_ref, plus_hbm, minus_hbm, rows, sems = refs
+    copies = [
+        pltpu.make_async_copy(field, hbm, sems.at[i])
+        for i, (field, hbm) in enumerate(zip(fields, (plus_hbm, minus_hbm)))
+    ]
+    for copy in copies:
+        copy.start()
     rows[...] = minus_ref[...].astype(F32)
     half = far_ref.shape[1] // 2
     receivers = w_ref.shape[1] // 2
@@ -201,6 +201,8 @@
         scaled = (part * scale).astype(BF16)
         for peer in range(peers):
             corr_ref[peer, c] = scaled[peer * each : (peer + 1) * each]
+    for copy in copies:
+        copy.wait()
 
 
 def total_kernel(got_ref, out_ref):
@@ -283,12 +285,11 @@
         return run(
             functools.partial(trace_kernel, n, not conj, conj, bool(extra)),
             (field_shape, send_shape(copies)),
-            [pltpu.VMEM(direct.shape, BF16), rows, rows, pltpu.SemaphoreType.DMA((n,))],
+            [rows, rows],
             summed,
             onset,
             table,
             *extra,
-            out_spaces=(pltpu.HBM, pltpu.VMEM),
         )
 
     summed = apply(plus)
@@ -306,14 +307,17 @@
     focus_plus, send = to_field(summed, False, halves, direct)
     plus = swap(send, OWNERS)
     each = focal // places
-    parts = run(
+    parts, focus_plus, focus_minus = run(
         functools.partial(green_kernel, 1.0 / receivers),
-        shape((places, 2, each, focal), BF16),
-        [pltpu.VMEM((2 * half, focal), F32)],
+        (shape((places, 2, each, focal), BF16), field_shape, field_shape),
+        [pltpu.VMEM((2 * half, focal), F32), pltpu.SemaphoreType.DMA((2,))],
         plus,
         w,
         w_far,
         minus.reshape(2 * half, focal),
+        focus_plus,
+        focus_minus,
+        out_spaces=(pltpu.VMEM, pltpu.HBM, pltpu.HBM),
     )
     correlation = run(
         total_kernel, shape((2, per_group, each, focal), F32), [], exchange(parts, RCV)

time: 162 us -> 161 us (level)
  no operation moved by 1% of the time
where the time goes in v2:
time: 161 us; the launch traced here: 160 us
  blocking collectives  82.4 us (51%)
  waiting for transfers between devices  34.5 us (21%)
  starting transfers between devices  30.3 us (19%)
  Pallas kernels  10.7 us (7%)
  local copies, waits for them, and re-layouts  1.79 us (1%)
    all_to_all x4, blocking collectives, exchange(): return lax.all_to_all(value, axes, split_axis=0, concat_axis=0, tiled=True)  82.4 us
    all_to_all x2, starting transfers between devices, exchange(): return lax.all_to_all(value, axes, split_axis=0, concat_axis=0, tiled=True)  23.4 us
    ppermute x3, waiting for transfers between devices, on_device(): got[d] = lax.ppermute(got[d], 'y', [(j, j ^ d) for j in range(ys)])  16.9 us
    all_to_all x2, waiting for transfers between devices, exchange(): return lax.all_to_all(value, axes, split_axis=0, concat_axis=0, tiled=True)  15.5 us
    pallas_call x9, Pallas kernels, run(): pl.pallas_call(kernel, out_shape=out, in_specs=[pl.BlockSpec(memory_space...  10.7 us
    ppermute x3, starting transfers between devices, on_device(): got[d] = lax.ppermute(got[d], 'y', [(j, j ^ d) for j in range(ys)])  4.79 us
  transfers between devices with their start and end apart: 6, of which 5 were waited for; matrix products, arithmetic and copies ran while one was open for 0% of the time, Pallas kernels for 1%

profile of v2, /device:TPU:2, one launch (start us, length us, event | category | flops | bytes accessed | tf_op | source)
XLA Modules:
  0.0 160.4 jit_solution(8216217469086572265)
XLA Ops:
  0.6 3.0 %shard_map.67 = (bf16[2,96,768]{2,1,0:T(8,128)(2,1)}, bf16[2,96,768]{2,1,0:T(8,128)(2,1)}, bf16[2,96,768]{2,1,0:T(8,128)(2,1)}, bf16[2,96,768]{2,1,0:T(8,128)(2,1)}, bf16[1,768,128]{2,1,0:T(8,128)(2,1)}) custom-call(bf16[2,4,96,768]{3,2,1,0:T(8,128)(2,1)} %reflection_hbm.1, bf16[3,128,512]{2,1,0:T(8,128)(2,1)} %refs_3_.1, ...), custom_call_target="tpu_custom_call" | custom-call | tf_op jit(solution)/shard_map/pallas_call | solution.py:35
  3.6 13.9 %all-to-all-start = ((bf16[128,3,2,128]{3,2,1,0:T(2,128)(2,1)}), bf16[128,3,2,128]{3,2,1,0:T(2,128)(2,1)S(1)}, u32[]{:S(2)}, u32[]{:S(2)}) async-start(bf16[128,3,2,128]{3,2,1,0:T(2,128)(2,1)} %bitcast.19), calls=%async_computation | async-start | bytes 393216 | tf_op jit(solution)/shard_map/all_to_all | solution.py:217
  17.5 1.7 %collective-permute-start = (bf16[2,96,768]{2,1,0:T(8,128)(2,1)}, bf16[2,96,768]{2,1,0:T(8,128)(2,1)S(1)}, u32[]{:S(2)}, u32[]{:S(2)}) collective-permute-start(bf16[2,96,768]{2,1,0:T(8,128)(2,1)} %get-tuple-element.23), channel_id=1, source_target_pairs={{0,1},{1,0},{2,3},{3,2},{4,5},{5,4},{6,7},{7,6},{8,9},{9,8},{10,11... | collective-permute-start | bytes 884744 | tf_op jit(solution)/shard_map/ppermute | solution.py:264
  19.2 3.1 %collective-permute-start.1 = (bf16[2,96,768]{2,1,0:T(8,128)(2,1)}, bf16[2,96,768]{2,1,0:T(8,128)(2,1)S(1)}, u32[]{:S(2)}, u32[]{:S(2)}) collective-permute-start(bf16[2,96,768]{2,1,0:T(8,128)(2,1)} %get-tuple-element.24), channel_id=1, source_target_pairs={{0,2},{1,3},{2,0},{3,1},{4,6},{5,7},{6,4},{7,5},{8,10},{9,11},{10,... | collective-permute-start | bytes 884744 | tf_op jit(solution)/shard_map/ppermute | solution.py:264
  22.3 0.0 collective-permute-start.2
  22.3 7.1 %collective-permute-done.refs_1_ = bf16[2,96,768]{2,1,0:T(8,128)(2,1)S(1)} collective-permute-done((bf16[2,96,768]{2,1,0:T(8,128)(2,1)}, bf16[2,96,768]{2,1,0:T(8,128)(2,1)S(1)}, u32[]{:S(2)}, u32[]{:S(2)}) %collective-permute-start) | collective-permute-done | bytes 294944 | tf_op jit(solution)/shard_map/ppermute | solution.py:264
  29.4 8.1 %collective-permute-done.1.refs_2_ = bf16[2,96,768]{2,1,0:T(8,128)(2,1)S(1)} collective-permute-done((bf16[2,96,768]{2,1,0:T(8,128)(2,1)}, bf16[2,96,768]{2,1,0:T(8,128)(2,1)S(1)}, u32[]{:S(2)}, u32[]{:S(2)}) %collective-permute-start.1) | collective-permute-done | bytes 294944 | tf_op jit(solution)/shard_map/ppermute | solution.py:264
  37.5 1.6 %collective-permute-done.2.refs_3_ = bf16[2,96,768]{2,1,0:T(8,128)(2,1)S(1)} collective-permute-done((bf16[2,96,768]{2,1,0:T(8,128)(2,1)}, bf16[2,96,768]{2,1,0:T(8,128)(2,1)S(1)}, u32[]{:S(2)}, u32[]{:S(2)}) %collective-permute-start.2) | collective-permute-done | bytes 294944 | tf_op jit(solution)/shard_map/ppermute | solution.py:264
  39.2 0.0 copy-start.2
  39.2 1.0 copy-done.2
  40.1 0.8 shard_map.68
  41.0 0.0 copy-start.4
  41.0 0.8 copy-done.4
  41.8 0.0 all-to-all-done
  41.8 0.0 copy-start
  41.8 0.0 copy-start.3
  41.8 1.4 shard_map.69
  43.2 9.5 %all-to-all-start.1 = ((bf16[256,3,2,128]{3,2,1,0:T(2,128)(2,1)}), bf16[256,3,2,128]{3,2,1,0:T(2,128)(2,1)S(1)}, u32[]{:S(2)}, u32[]{:S(2)}) async-start(bf16[256,3,2,128]{3,2,1,0:T(2,128)(2,1)} %bitcast.2), calls=%async_computation.1 | async-start | bytes 786432 | tf_op jit(solution)/shard_map/all_to_all | solution.py:217
  52.7 2.2 %collective-permute-start.3 = (bf16[4,2,96,384]{3,2,1,0:T(8,128)(2,1)}, bf16[4,2,96,384]{3,2,1,0:T(8,128)(2,1)}, u32[]{:S(2)}, u32[]{:S(2)}) collective-permute-start(bf16[4,2,96,384]{3,2,1,0:T(8,128)(2,1)} %copy-done.4), channel_id=1, source_target_pairs={{0,4},{4,0},{1,5},{5,1},{2,6},{6,2},{3,7},{7,3},{8,12},{12,8},{9,1... | collective-permute-start | bytes 1769480 | tf_op jit(solution)/shard_map/ppermute | solution.py:272
  54.8 15.5 %all-to-all-done.1 = bf16[256,3,2,128]{3,2,1,0:T(2,128)(2,1)S(1)} async-done(((bf16[256,3,2,128]{3,2,1,0:T(2,128)(2,1)}), bf16[256,3,2,128]{3,2,1,0:T(2,128)(2,1)S(1)}, u32[]{:S(2)}, u32[]{:S(2)}) %all-to-all-start.1) | async-done | bytes 393248 | tf_op jit(solution)/shard_map/all_to_all | solution.py:217
  70.3 0.0 copy-done
  70.3 0.0 copy-done.3
  70.3 0.8 shard_map.70
  71.1 2.1 %collective-permute-done.3.cut_ref = bf16[4,2,96,384]{3,2,1,0:T(8,128)(2,1)} collective-permute-done((bf16[4,2,96,384]{3,2,1,0:T(8,128)(2,1)}, bf16[4,2,96,384]{3,2,1,0:T(8,128)(2,1)}, u32[]{:S(2)}, u32[]{:S(2)}) %collective-permute-start.3) | collective-permute-done | bytes 589856 | tf_op jit(solution)/shard_map/ppermute | solution.py:272
  73.3 1.4 shard_map.71.refs_2_
  74.7 23.9 %all_to_all.30 = bf16[128,3,2,128]{3,2,1,0:T(2,128)(2,1)S(1)} all-to-all(bf16[128,3,2,128]{3,2,1,0:T(2,128)(2,1)S(1)} %bitcast.18), channel_id=1, replica_groups=mesh['freq'=32,'xh'=2,'y'=4] {'y','freq'}, dimensions={0} | all-to-all | bytes 393216 | tf_op jit(solution)/shard_map/all_to_all | solution.py:217
  98.7 0.0 copy-start.1
  98.7 0.6 shard_map.72
  99.3 24.1 %all_to_all.31 = bf16[256,3,2,128]{3,2,1,0:T(2,128)(2,1)S(1)} all-to-all(bf16[256,3,2,128]{3,2,1,0:T(2,128)(2,1)S(1)} %bitcast.15), channel_id=1, replica_groups=mesh['freq'=32,'xh'=2,'y'=4] {'xh','y','freq'}, dimensions={0} | all-to-all | bytes 786432 | tf_op jit(solution)/shard_map/all_to_all | solution.py:217
  123.4 0.0 copy-done.1
  123.4 0.9 shard_map.73
  124.3 24.0 %all_to_all.32 = bf16[256,3,2,128]{3,2,1,0:T(2,128)(2,1)S(1)} all-to-all(bf16[256,3,2,128]{3,2,1,0:T(2,128)(2,1)S(1)} %bitcast.17), channel_id=1, replica_groups=mesh['freq'=32,'xh'=2,'y'=4] {'xh','y','freq'}, dimensions={0} | all-to-all | bytes 786432 | tf_op jit(solution)/shard_map/all_to_all | solution.py:217
  148.2 1.1 shard_map.74
  149.4 10.4 %all_to_all.33.got_ref = bf16[8,2,16,128]{3,2,1,0:T(8,128)(2,1)S(1)} all-to-all(bf16[8,2,16,128]{3,2,1,0:T(8,128)(2,1)S(1)} %get-tuple-element.38), channel_id=1, replica_groups=mesh['freq'=32,'xh'=2,'y'=4] {'xh','y'}, dimensions={0} | all-to-all | bytes 131072 | tf_op jit(solution)/shard_map/all_to_all | solution.py:217
  159.8 0.6 shard_map.75
Async XLA Ops:
  3.6 38.2 %all-to-all-start = ((bf16[128,3,2,128]{3,2,1,0:T(2,128)(2,1)}), bf16[128,3,2,128]{3,2,1,0:T(2,128)(2,1)S(1)}, u32[]{:S(2)}, u32[]{:S(2)}) async-start(bf16[128,3,2,128]{3,2,1,0:T(2,128)(2,1)} %bitcast.19), calls=%async_computation | async-start | bytes 393216 | tf_op jit(solution)/shard_map/all_to_all | solution.py:217
  17.5 11.9 %collective-permute-start = (bf16[2,96,768]{2,1,0:T(8,128)(2,1)}, bf16[2,96,768]{2,1,0:T(8,128)(2,1)S(1)}, u32[]{:S(2)}, u32[]{:S(2)}) collective-permute-start(bf16[2,96,768]{2,1,0:T(8,128)(2,1)} %get-tuple-element.23), channel_id=1, source_target_pairs={{0,1},{1,0},{2,3},{3,2},{4,5},{5,4},{6,7},{7,6},{8,9},{9,8},{10,11... | collective-permute-start | bytes 884744 | tf_op jit(solution)/shard_map/ppermute | solution.py:264
  19.2 18.3 %collective-permute-start.1 = (bf16[2,96,768]{2,1,0:T(8,128)(2,1)}, bf16[2,96,768]{2,1,0:T(8,128)(2,1)S(1)}, u32[]{:S(2)}, u32[]{:S(2)}) collective-permute-start(bf16[2,96,768]{2,1,0:T(8,128)(2,1)} %get-tuple-element.24), channel_id=1, source_target_pairs={{0,2},{1,3},{2,0},{3,1},{4,6},{5,7},{6,4},{7,5},{8,10},{9,11},{10,... | collective-permute-start | bytes 884744 | tf_op jit(solution)/shard_map/ppermute | solution.py:264
  22.3 16.9 %collective-permute-start.2 = (bf16[2,96,768]{2,1,0:T(8,128)(2,1)}, bf16[2,96,768]{2,1,0:T(8,128)(2,1)S(1)}, u32[]{:S(2)}, u32[]{:S(2)}) collective-permute-start(bf16[2,96,768]{2,1,0:T(8,128)(2,1)} %get-tuple-element.25), channel_id=1, source_target_pairs={{0,3},{1,2},{2,1},{3,0},{4,7},{5,6},{6,5},{7,4},{8,11},{9,10},{10,... | collective-permute-start | bytes 884744 | tf_op jit(solution)/shard_map/ppermute | solution.py:264
  39.2 1.0 copy-start.2
  41.0 0.8 copy-start.4
  41.8 28.5 %copy-start = (bf16[256,512]{1,0:T(8,128)(2,1)S(1)}, bf16[256,512]{1,0:T(8,128)(2,1)}, u32[]{:S(2)}) copy-start(bf16[256,512]{1,0:T(8,128)(2,1)} %constant.2.clone.table_hbm.refs_2_) | copy-start | bytes 786436
  41.8 28.5 %copy-start.3 = (s32[3,128]{1,0:T(4,128)S(1)}, s32[3,128]{1,0:T(4,128)}, u32[]{:S(2)}) copy-start(s32[3,128]{1,0:T(4,128)} %refs_1_.3) | copy-start | bytes 4612
  43.2 27.1 %all-to-all-start.1 = ((bf16[256,3,2,128]{3,2,1,0:T(2,128)(2,1)}), bf16[256,3,2,128]{3,2,1,0:T(2,128)(2,1)S(1)}, u32[]{:S(2)}, u32[]{:S(2)}) async-start(bf16[256,3,2,128]{3,2,1,0:T(2,128)(2,1)} %bitcast.2), calls=%async_computation.1 | async-start | bytes 786432 | tf_op jit(solution)/shard_map/all_to_all | solution.py:217
  52.7 20.6 %collective-permute-start.3 = (bf16[4,2,96,384]{3,2,1,0:T(8,128)(2,1)}, bf16[4,2,96,384]{3,2,1,0:T(8,128)(2,1)}, u32[]{:S(2)}, u32[]{:S(2)}) collective-permute-start(bf16[4,2,96,384]{3,2,1,0:T(8,128)(2,1)} %copy-done.4), channel_id=1, source_target_pairs={{0,4},{4,0},{1,5},{5,1},{2,6},{6,2},{3,7},{7,3},{8,12},{12,8},{9,1... | collective-permute-start | bytes 1769480 | tf_op jit(solution)/shard_map/ppermute | solution.py:272
  98.7 24.8 %copy-start.1 = (bf16[3,128,512]{2,1,0:T(8,128)(2,1)S(1)}, bf16[3,128,512]{2,1,0:T(8,128)(2,1)}, u32[]{:S(2)}) copy-start(bf16[3,128,512]{2,1,0:T(8,128)(2,1)} %refs_3_.1) | copy-start | bytes 1179652

commit v3 on v2

--- a/solution.py
+++ b/solution.py
@@ -69,20 +69,19 @@
     ]
     takes, puts = [], []
     for d, block_hbm in enumerate(block_hbms):
-        at = jnp.bitwise_xor(y, d)
+        at = jnp.bitwise_xor(y, d + 1)
         sem = in_sems.at[1 + n + d]
         takes.append(pltpu.make_async_copy(reflection_hbm.at[:, at], blocks_ref.at[d], sem))
         puts.append(pltpu.make_async_copy(blocks_ref.at[d], block_hbm, out_sems.at[d]))
-    for copy in (whole, *parts, *takes):
+    for copy in (*takes, whole, *parts):
         copy.start()
+    for take, put in zip(takes, puts):
+        take.wait()
+        put.start()
     whole.wait()
     for i in range(n):
         parts[i].wait()
         put_spectrum(direct_ref[i], table_ref[...], out_rows, i, 2 * n, False)
-        if i == 0:
-            for take, put in zip(takes, puts):
-                take.wait()
-                put.start()
     flush(out_rows, send_ref)
     for put in puts:
         put.wait()
@@ -126,14 +125,15 @@
 
 
 def weave_sources_kernel(*refs):
-    *got_refs, w_ref, cut_ref, even_odd = refs
+    reflection_ref, *got_refs, w_ref, cut_ref, even_odd = refs
     _, block, receivers = got_refs[0].shape
     lanes = even_odd.shape[1]
     half = cut_ref.shape[3]
     other = pl.multiple_of((1 - lax.axis_index("xh")) * half, half)
+    y = lax.axis_index("y")
+    got_refs = [reflection_ref.at[:, y], *got_refs]
     for d, ref in enumerate(got_refs):
         cut_ref[d] = ref[:, :, pl.ds(other, half)]
-    y = lax.axis_index("y")
     starts = [2 * block * jnp.bitwise_xor(y, d) for d in range(len(got_refs))]
     for out in (0, 1):
         for col in range(0, receivers, lanes):
@@ -190,12 +190,13 @@
     def part(c):
         cols = pl.ds(pl.multiple_of(c * receivers + xh * half, half), half)
         near = dot(own, w_ref[:, cols], 0, 0)
-        return (near + dot(far, far_ref[:, c * half : (c + 1) * half], 0, 0)).T
-
-    re = (part(0) - rows[pl.ds(0, half, stride=2), :]).astype(BF16)
-    im = (part(1) + rows[pl.ds(1, half, stride=2), :]).astype(BF16)
-    cross = dot(re, im, 0, 0)
-    parts = (dot(re, re, 0, 0) + dot(im, im, 0, 0), cross - cross.T)
+        return near + dot(far, far_ref[:, c * half : (c + 1) * half], 0, 0)
+
+    minus_re, minus_im = rows[pl.ds(0, half, stride=2), :].T, rows[pl.ds(1, half, stride=2), :].T
+    re = (part(0) - minus_re).astype(BF16)
+    im = (part(1) + minus_im).astype(BF16)
+    cross = dot(re, im, 1, 1)
+    parts = (dot(re, re, 1, 1) + dot(im, im, 1, 1), cross - cross.T)
     peers, _, each, _ = corr_ref.shape
     for c, part in enumerate(parts):
         scaled = (part * scale).astype(BF16)
@@ -245,28 +246,29 @@
     piece = shape((2, block, receivers), BF16)
     *got, send = run(
         open_kernel,
-        [piece] * ys + [send_shape(1)],
+        [piece] * (ys - 1) + [send_shape(1)],
         [
-            pltpu.VMEM((ys, *piece.shape), BF16),
+            pltpu.VMEM((ys - 1, *piece.shape), BF16),
             pltpu.VMEM(direct.shape, BF16),
             pltpu.VMEM(table.shape, BF16),
             rows,
-            pltpu.SemaphoreType.DMA((1 + n + ys,)),
-            pltpu.SemaphoreType.DMA((ys,)),
+            pltpu.SemaphoreType.DMA((n + ys,)),
+            pltpu.SemaphoreType.DMA((ys - 1,)),
         ],
         reflection,
         direct,
         table,
         space=pltpu.HBM,
-        out_spaces=[pltpu.HBM] * ys + [pltpu.VMEM],
+        out_spaces=[pltpu.HBM] * (ys - 1) + [pltpu.VMEM],
     )
     for d in range(1, ys):
-        got[d] = lax.ppermute(got[d], "y", [(j, j ^ d) for j in range(ys)])
+        got[d - 1] = lax.ppermute(got[d - 1], "y", [(j, j ^ d) for j in range(ys)])
     plus = swap(send, TRACES)
     w, cut = run(
         weave_sources_kernel,
         (shape((2 * half, 2 * receivers), BF16), shape((ys, 2, block, half), BF16)),
         [pltpu.VMEM((2 * half, focal), F32)],
+        reflection,
         *got,
     )
     far = lax.ppermute(cut, "xh", [(j, j ^ 1) for j in range(halves)])

time: 161 us -> 161 us (level)
  no operation moved by 1% of the time
where the time goes in v3:
time: 161 us; the launch traced here: 160 us
  blocking collectives  82.4 us (51%)
  waiting for transfers between devices  34.5 us (21%)
  starting transfers between devices  30.3 us (19%)
  Pallas kernels  10.3 us (6%)
  local copies, waits for them, and re-layouts  2.1 us (1%)
    all_to_all x4, blocking collectives, exchange(): return lax.all_to_all(value, axes, split_axis=0, concat_axis=0, tiled=True)  82.4 us
    all_to_all x2, starting transfers between devices, exchange(): return lax.all_to_all(value, axes, split_axis=0, concat_axis=0, tiled=True)  23.4 us
    ppermute x3, waiting for transfers between devices, on_device(): got[d - 1] = lax.ppermute(got[d - 1], 'y', [(j, j ^ d) for j in range(ys)])  16.9 us
    all_to_all x2, waiting for transfers between devices, exchange(): return lax.all_to_all(value, axes, split_axis=0, concat_axis=0, tiled=True)  15.5 us
    pallas_call x9, Pallas kernels, run(): pl.pallas_call(kernel, out_shape=out, in_specs=[pl.BlockSpec(memory_space...  10.3 us
    ppermute x3, starting transfers between devices, on_device(): got[d - 1] = lax.ppermute(got[d - 1], 'y', [(j, j ^ d) for j in range(ys)])  4.79 us
  transfers between devices with their start and end apart: 6, of which 5 were waited for; matrix products, arithmetic and copies ran while one was open for 0% of the time, Pallas kernels for 1%

profile of v3, /device:TPU:2, one launch (start us, length us, event | category | flops | bytes accessed | tf_op | source)
XLA Modules:
  0.0 160.4 jit_solution(3455696998870712683)
XLA Ops:
  0.6 2.8 %shard_map.67 = (bf16[2,96,768]{2,1,0:T(8,128)(2,1)}, bf16[2,96,768]{2,1,0:T(8,128)(2,1)}, bf16[2,96,768]{2,1,0:T(8,128)(2,1)}, bf16[1,768,128]{2,1,0:T(8,128)(2,1)}) custom-call(bf16[2,4,96,768]{3,2,1,0:T(8,128)(2,1)} %refs_0_.1, bf16[3,128,512]{2,1,0:T(8,128)(2,1)} %refs_3_.1, bf16[256,512]{1,0:T(8,128)(2,1)} %constant.2.clone.table_hbm.refs_2_), custom_call_target="tpu_custom_call" | custom-call | tf_op jit(solution)/shard_map/pallas_call | solution.py:35
  3.5 13.9 %all-to-all-start = ((bf16[128,3,2,128]{3,2,1,0:T(2,128)(2,1)}), bf16[128,3,2,128]{3,2,1,0:T(2,128)(2,1)S(1)}, u32[]{:S(2)}, u32[]{:S(2)}) async-start(bf16[128,3,2,128]{3,2,1,0:T(2,128)(2,1)} %bitcast.19), calls=%async_computation | async-start | bytes 393216 | tf_op jit(solution)/shard_map/all_to_all | solution.py:218
  17.4 1.7 %collective-permute-start = (bf16[2,96,768]{2,1,0:T(8,128)(2,1)}, bf16[2,96,768]{2,1,0:T(8,128)(2,1)S(1)}, u32[]{:S(2)}, u32[]{:S(2)}) collective-permute-start(bf16[2,96,768]{2,1,0:T(8,128)(2,1)} %get-tuple-element.21), channel_id=1, source_target_pairs={{0,1},{1,0},{2,3},{3,2},{4,5},{5,4},{6,7},{7,6},{8,9},{9,8},{10,11... | collective-permute-start | bytes 884744 | tf_op jit(solution)/shard_map/ppermute | solution.py:265
  19.1 3.1 %collective-permute-start.1 = (bf16[2,96,768]{2,1,0:T(8,128)(2,1)}, bf16[2,96,768]{2,1,0:T(8,128)(2,1)S(1)}, u32[]{:S(2)}, u32[]{:S(2)}) collective-permute-start(bf16[2,96,768]{2,1,0:T(8,128)(2,1)} %get-tuple-element.22), channel_id=1, source_target_pairs={{0,2},{1,3},{2,0},{3,1},{4,6},{5,7},{6,4},{7,5},{8,10},{9,11},{10,... | collective-permute-start | bytes 884744 | tf_op jit(solution)/shard_map/ppermute | solution.py:265
  22.2 0.0 collective-permute-start.2
  22.2 7.1 %collective-permute-done.refs_1_ = bf16[2,96,768]{2,1,0:T(8,128)(2,1)S(1)} collective-permute-done((bf16[2,96,768]{2,1,0:T(8,128)(2,1)}, bf16[2,96,768]{2,1,0:T(8,128)(2,1)S(1)}, u32[]{:S(2)}, u32[]{:S(2)}) %collective-permute-start) | collective-permute-done | bytes 294944 | tf_op jit(solution)/shard_map/ppermute | solution.py:265
  29.2 8.1 %collective-permute-done.1.refs_2_ = bf16[2,96,768]{2,1,0:T(8,128)(2,1)S(1)} collective-permute-done((bf16[2,96,768]{2,1,0:T(8,128)(2,1)}, bf16[2,96,768]{2,1,0:T(8,128)(2,1)S(1)}, u32[]{:S(2)}, u32[]{:S(2)}) %collective-permute-start.1) | collective-permute-done | bytes 294944 | tf_op jit(solution)/shard_map/ppermute | solution.py:265
  37.4 1.6 %collective-permute-done.2.refs_3_ = bf16[2,96,768]{2,1,0:T(8,128)(2,1)S(1)} collective-permute-done((bf16[2,96,768]{2,1,0:T(8,128)(2,1)}, bf16[2,96,768]{2,1,0:T(8,128)(2,1)S(1)}, u32[]{:S(2)}, u32[]{:S(2)}) %collective-permute-start.2) | collective-permute-done | bytes 294944 | tf_op jit(solution)/shard_map/ppermute | solution.py:265
  39.0 0.0 copy-start
  39.0 1.3 copy-done
  40.3 0.8 shard_map.68
  41.1 0.0 copy-start.4
  41.1 0.8 copy-done.4
  41.9 0.0 all-to-all-done
  42.0 0.0 copy-start.1
  42.0 0.0 copy-start.3
  42.0 1.4 shard_map.69
  43.4 9.5 %all-to-all-start.1 = ((bf16[256,3,2,128]{3,2,1,0:T(2,128)(2,1)}), bf16[256,3,2,128]{3,2,1,0:T(2,128)(2,1)S(1)}, u32[]{:S(2)}, u32[]{:S(2)}) async-start(bf16[256,3,2,128]{3,2,1,0:T(2,128)(2,1)} %bitcast.2), calls=%async_computation.1 | async-start | bytes 786432 | tf_op jit(solution)/shard_map/all_to_all | solution.py:218
  52.8 2.2 %collective-permute-start.3 = (bf16[4,2,96,384]{3,2,1,0:T(8,128)(2,1)}, bf16[4,2,96,384]{3,2,1,0:T(8,128)(2,1)}, u32[]{:S(2)}, u32[]{:S(2)}) collective-permute-start(bf16[4,2,96,384]{3,2,1,0:T(8,128)(2,1)} %copy-done.4), channel_id=1, source_target_pairs={{0,4},{4,0},{1,5},{5,1},{2,6},{6,2},{3,7},{7,3},{8,12},{12,8},{9,1... | collective-permute-start | bytes 1769480 | tf_op jit(solution)/shard_map/ppermute | solution.py:274
  55.0 15.5 %all-to-all-done.1 = bf16[256,3,2,128]{3,2,1,0:T(2,128)(2,1)S(1)} async-done(((bf16[256,3,2,128]{3,2,1,0:T(2,128)(2,1)}), bf16[256,3,2,128]{3,2,1,0:T(2,128)(2,1)S(1)}, u32[]{:S(2)}, u32[]{:S(2)}) %all-to-all-start.1) | async-done | bytes 393248 | tf_op jit(solution)/shard_map/all_to_all | solution.py:218
  70.5 0.0 copy-done.1
  70.5 0.0 copy-done.3
  70.5 0.8 shard_map.70
  71.3 2.1 %collective-permute-done.3.cut_ref = bf16[4,2,96,384]{3,2,1,0:T(8,128)(2,1)} collective-permute-done((bf16[4,2,96,384]{3,2,1,0:T(8,128)(2,1)}, bf16[4,2,96,384]{3,2,1,0:T(8,128)(2,1)}, u32[]{:S(2)}, u32[]{:S(2)}) %collective-permute-start.3) | collective-permute-done | bytes 589856 | tf_op jit(solution)/shard_map/ppermute | solution.py:274
  73.4 1.4 shard_map.71.refs_2_
  74.9 23.9 %all_to_all.30 = bf16[128,3,2,128]{3,2,1,0:T(2,128)(2,1)S(1)} all-to-all(bf16[128,3,2,128]{3,2,1,0:T(2,128)(2,1)S(1)} %bitcast.18), channel_id=1, replica_groups=mesh['freq'=32,'xh'=2,'y'=4] {'y','freq'}, dimensions={0} | all-to-all | bytes 393216 | tf_op jit(solution)/shard_map/all_to_all | solution.py:218
  98.8 0.0 copy-start.2
  98.8 0.6 shard_map.72
  99.5 24.1 %all_to_all.31 = bf16[256,3,2,128]{3,2,1,0:T(2,128)(2,1)S(1)} all-to-all(bf16[256,3,2,128]{3,2,1,0:T(2,128)(2,1)S(1)} %bitcast.15), channel_id=1, replica_groups=mesh['freq'=32,'xh'=2,'y'=4] {'xh','y','freq'}, dimensions={0} | all-to-all | bytes 786432 | tf_op jit(solution)/shard_map/all_to_all | solution.py:218
  123.6 0.0 copy-done.2
  123.6 0.8 shard_map.73
  124.4 24.0 %all_to_all.32 = bf16[256,3,2,128]{3,2,1,0:T(2,128)(2,1)S(1)} all-to-all(bf16[256,3,2,128]{3,2,1,0:T(2,128)(2,1)S(1)} %bitcast.17), channel_id=1, replica_groups=mesh['freq'=32,'xh'=2,'y'=4] {'xh','y','freq'}, dimensions={0} | all-to-all | bytes 786432 | tf_op jit(solution)/shard_map/all_to_all | solution.py:218
  148.4 0.9 shard_map.74
  149.3 10.4 %all_to_all.33.got_ref = bf16[8,2,16,128]{3,2,1,0:T(8,128)(2,1)S(1)} all-to-all(bf16[8,2,16,128]{3,2,1,0:T(8,128)(2,1)S(1)} %get-tuple-element.36), channel_id=1, replica_groups=mesh['freq'=32,'xh'=2,'y'=4] {'xh','y'}, dimensions={0} | all-to-all | bytes 131072 | tf_op jit(solution)/shard_map/all_to_all | solution.py:218
  159.7 0.6 shard_map.75
Async XLA Ops:
  3.5 38.5 %all-to-all-start = ((bf16[128,3,2,128]{3,2,1,0:T(2,128)(2,1)}), bf16[128,3,2,128]{3,2,1,0:T(2,128)(2,1)S(1)}, u32[]{:S(2)}, u32[]{:S(2)}) async-start(bf16[128,3,2,128]{3,2,1,0:T(2,128)(2,1)} %bitcast.19), calls=%async_computation | async-start | bytes 393216 | tf_op jit(solution)/shard_map/all_to_all | solution.py:218
  17.4 11.9 %collective-permute-start = (bf16[2,96,768]{2,1,0:T(8,128)(2,1)}, bf16[2,96,768]{2,1,0:T(8,128)(2,1)S(1)}, u32[]{:S(2)}, u32[]{:S(2)}) collective-permute-start(bf16[2,96,768]{2,1,0:T(8,128)(2,1)} %get-tuple-element.21), channel_id=1, source_target_pairs={{0,1},{1,0},{2,3},{3,2},{4,5},{5,4},{6,7},{7,6},{8,9},{9,8},{10,11... | collective-permute-start | bytes 884744 | tf_op jit(solution)/shard_map/ppermute | solution.py:265
  19.1 18.3 %collective-permute-start.1 = (bf16[2,96,768]{2,1,0:T(8,128)(2,1)}, bf16[2,96,768]{2,1,0:T(8,128)(2,1)S(1)}, u32[]{:S(2)}, u32[]{:S(2)}) collective-permute-start(bf16[2,96,768]{2,1,0:T(8,128)(2,1)} %get-tuple-element.22), channel_id=1, source_target_pairs={{0,2},{1,3},{2,0},{3,1},{4,6},{5,7},{6,4},{7,5},{8,10},{9,11},{10,... | collective-permute-start | bytes 884744 | tf_op jit(solution)/shard_map/ppermute | solution.py:265
  22.2 16.9 %collective-permute-start.2 = (bf16[2,96,768]{2,1,0:T(8,128)(2,1)}, bf16[2,96,768]{2,1,0:T(8,128)(2,1)S(1)}, u32[]{:S(2)}, u32[]{:S(2)}) collective-permute-start(bf16[2,96,768]{2,1,0:T(8,128)(2,1)} %get-tuple-element.23), channel_id=1, source_target_pairs={{0,3},{1,2},{2,1},{3,0},{4,7},{5,6},{6,5},{7,4},{8,11},{9,10},{10,... | collective-permute-start | bytes 884744 | tf_op jit(solution)/shard_map/ppermute | solution.py:265
  39.0 1.3 copy-start
  41.1 0.8 copy-start.4
  42.0 28.5 %copy-start.1 = (bf16[256,512]{1,0:T(8,128)(2,1)S(1)}, bf16[256,512]{1,0:T(8,128)(2,1)}, u32[]{:S(2)}) copy-start(bf16[256,512]{1,0:T(8,128)(2,1)} %constant.2.clone.table_hbm.refs_2_) | copy-start | bytes 786436
  42.0 28.5 %copy-start.3 = (s32[3,128]{1,0:T(4,128)S(1)}, s32[3,128]{1,0:T(4,128)}, u32[]{:S(2)}) copy-start(s32[3,128]{1,0:T(4,128)} %refs_1_.3) | copy-start | bytes 4612
  43.4 27.1 %all-to-all-start.1 = ((bf16[256,3,2,128]{3,2,1,0:T(2,128)(2,1)}), bf16[256,3,2,128]{3,2,1,0:T(2,128)(2,1)S(1)}, u32[]{:S(2)}, u32[]{:S(2)}) async-start(bf16[256,3,2,128]{3,2,1,0:T(2,128)(2,1)} %bitcast.2), calls=%async_computation.1 | async-start | bytes 786432 | tf_op jit(solution)/shard_map/all_to_all | solution.py:218
  52.8 20.6 %collective-permute-start.3 = (bf16[4,2,96,384]{3,2,1,0:T(8,128)(2,1)}, bf16[4,2,96,384]{3,2,1,0:T(8,128)(2,1)}, u32[]{:S(2)}, u32[]{:S(2)}) collective-permute-start(bf16[4,2,96,384]{3,2,1,0:T(8,128)(2,1)} %copy-done.4), channel_id=1, source_target_pairs={{0,4},{4,0},{1,5},{5,1},{2,6},{6,2},{3,7},{7,3},{8,12},{12,8},{9,1... | collective-permute-start | bytes 1769480 | tf_op jit(solution)/shard_map/ppermute | solution.py:274
  98.8 24.8 %copy-start.2 = (bf16[3,128,512]{2,1,0:T(8,128)(2,1)S(1)}, bf16[3,128,512]{2,1,0:T(8,128)(2,1)}, u32[]{:S(2)}) copy-start(bf16[3,128,512]{2,1,0:T(8,128)(2,1)} %refs_3_.1) | copy-start | bytes 1179652
